TPU v7x, 128 devices: a whole 4x4x4 slice. The times are simulated.
128 devices in a mesh: blk: 32 (over z, y_hi, x), field: 4 (over y_lo, core).
Axes of the slice: x: 4, y: 4 (y_hi: 2, y_lo: 2; y = y_hi * 2 + y_lo), z: 4, core: 2. Of those that a mesh axis runs over, the one named last changes fastest.
Arguments:
- vectors: float32 [2048, 32768], P('blk', 'field'), may hold values from 0 to 10
- section: int32 [1], replicated, may hold values from 0 to 31
Outputs:
- metrics: float32 [2048, 4, 64], P('blk', None, 'field')
All inputs are finite; a program needn't handle non-finite values.
Results may differ from a plain program's by a relative error of at most 0.0003.
Values sent between devices are 32-bit elements; how exact they have to be, the bound alone decides.
A program may use at most 64 MiB of HBM per device.

v0:
```python
import jax
import jax.numpy as jnp
from jax import lax
from jax.experimental import pallas as pl
from jax.experimental.pallas import tpu as pltpu
from jax.sharding import Mesh
from jax.sharding import PartitionSpec as P

MESH = pl.DeviceIdType.MESH
AXES = ("z", "yh", "x", "yl", "core")
ROUNDS = 4
HALF = 128 // ROUNDS
NF = 2 * HALF
PITCH = NF + 8
TILES = 16
VREG = (8, 128)


def iota(axis):
    return lax.broadcasted_iota(jnp.int32, VREG, axis)


def spread(row):
    return jnp.broadcast_to(row, VREG)


def take(value, index):
    return jnp.take_along_axis(value, index, axis=1)


def kernel(
    section, x_hbm, out, xin, sent, got, rows, cols, roll_a, roll_b, acc, sums, core_in, plane_in, column_out, column_in,
    turn, load_sem, a_send, a_recv, c_send, c_recv, p_send, p_recv, y_send, y_recv,
):
    z, yh, x, yl, core = (lax.axis_index(name) for name in AXES)
    offset = section[0]
    block = z * 8 + yh * 4 + x
    column = yh * 2 + yl

    def blk_peer(e):
        return (lax.rem(z + e // 8, 4), lax.rem(yh + (e // 4) % 2, 2), lax.rem(x + e % 4, 4), yl, core)

    def plane_peer(e):
        return (lax.rem(z + e // 4, 4), yh, lax.rem(x + e % 4, 4), yl, core)

    def column_peer(d):
        y = lax.rem(column + d, 4)
        return (z, y // 2, x, lax.rem(y, 2), core)

    other_core = (z, yh, x, yl, 1 - core)

    loads = []
    for i in range(8):
        part = pl.ds(i * 1024, 1024)
        loads.append(pltpu.make_async_copy(x_hbm.at[:, part], xin.at[:, part], load_sem.at[i]))
        loads[-1].start()

    barrier = pltpu.get_barrier_semaphore()
    for e in range(1, 32):
        pl.semaphore_signal(barrier, inc=1, device_id=blk_peer(e), device_id_type=MESH)
    for peer in (column_peer(1), column_peer(3), other_core):
        pl.semaphore_signal(barrier, inc=1, device_id=peer, device_id_type=MESH)

    lane, sub = iota(1), iota(0)
    lane_c, lane_rho, lane_h = lane // 8, (lane // 2) % 4, lane % 2
    row_index = [lane_h * 64 + lane_rho * 16 + (lane_c + sub + 8 * q) % 16 for q in range(2)]
    col_index = [lane_h * 64 + g * 16 + lane_c for g in range(4)]

    for load in loads:
        load.wait()

    def transpose_one(u, _):
        left = xin[:, pl.ds(pl.multiple_of(u * 128, 128), 128)]
        right = xin[:, pl.ds(pl.multiple_of(u * 128 + 4096, 128), 128)]
        sent[u] = jnp.concatenate([left, right], axis=0).T
        return 0

    lax.fori_loop(0, 32, transpose_one, 0)
    got[block] = sent[block]
    for tile in range(32):
        sums[tile] = jnp.zeros(VREG, jnp.float32)

    def clear(tile, _):
        for c in range(2):
            for a in range(16):
                acc[tile, c, a] = jnp.zeros(VREG, jnp.float32)
        return 0

    lax.fori_loop(0, TILES, clear, 0)
    pl.semaphore_wait(barrier, 34)

    def a_copy(j, e):
        z2, yh2, x2, _, _ = blk_peer(e)
        part = pl.ds(pl.multiple_of(j * HALF, HALF), HALF)
        return pltpu.make_async_remote_copy(
            src_ref=sent.at[z2 * 8 + yh2 * 4 + x2, part],
            dst_ref=got.at[block, part],
            send_sem=a_send.at[j, e],
            recv_sem=a_recv.at[j, e],
            device_id=blk_peer(e),
            device_id_type=MESH,
        )

    def send_round(j, _):
        def send_one(i, _):
            a_copy(j, lax.rem(i * 13, 32)).start()
            return 0

        lax.fori_loop(1, 32, send_one, 0)
        return 0

    lax.fori_loop(0, ROUNDS, send_round, 0)

    def tile_at(i):
        e = lax.rem((15 - i) * 7, 16)
        return e, lax.rem(z + e // 4, 4) * 4 + lax.rem(x + e % 4, 4)

    def first_block(tile):
        return (tile // 4) * 8 + lax.rem(tile, 4)

    def arrange(j):
        def one(t, _):
            t4 = lax.rem(t + 4, 32)
            total = sums[t]
            for o in range(HALF // 8):
                part = pl.ds(pl.multiple_of(j * HALF + o * 8, 8), 8)
                a, b = got[t, part, :], got[t4, part, :]
                for h, pair in enumerate(
                    (jnp.where(lane < 64, a, pltpu.roll(b, 64, 1)), jnp.where(lane < 64, pltpu.roll(a, 64, 1), b))
                ):
                    at = h * HALF + o * 8
                    total = total + pair
                    rows[t, pl.ds(at, 8), :] = pair
                    for g in range(4):
                        cols[t, pl.ds(g * PITCH + at, 8), :] = take(pair, col_index[g])
            sums[t] = total
            return 0

        lax.fori_loop(0, 32, one, 0)

    def turn_field(target, r, f):
        row = spread(rows[r, pl.ds(f, 1), :])
        for q in range(2):
            target[f, q] = take(row, row_index[q])

    def work(i, now, later):
        _, tile = tile_at(i)
        r = first_block(tile)
        follow = first_block(tile_at(lax.rem(i + 1, TILES))[1])
        partner = [lax.rem(r + offset + s, 32) for s in range(4)]
        total = [[acc[tile, a // 16, a % 16]] for a in range(32)]
        for f in range(NF):
            turned = [now[f, q] for q in range(2)]
            for s in range(4):
                for g in range(4):
                    other = spread(cols[partner[s], pl.ds(g * PITCH + f, 1), :])
                    for q in range(2):
                        a = (g % 2) * 16 + (g // 2) * 8 + s * 2 + q
                        total[a][0] = total[a][0] + jnp.minimum(turned[q], other)
            turn_field(later, follow, f)
        for a in range(32):
            acc[tile, a // 16, a % 16] = total[a][0]

    def ready(j):
        def wait_one(i, _):
            a_copy(j, lax.rem(i * 13, 32)).wait_recv()
            return 0

        lax.fori_loop(1, 32, wait_one, 0)
        arrange(j)
        r0 = first_block(tile_at(0)[1])

        def first(b, _):
            for f in range(8):
                turn_field(roll_a, r0, b * 8 + f)
            return 0

        lax.fori_loop(0, NF // 8, first, 0)

    def round_of(j, _):
        ready(j)

        def two(i, _):
            work(2 * i, roll_a, roll_b)
            work(2 * i + 1, roll_b, roll_a)
            return 0

        lax.fori_loop(0, TILES // 2, two, 0)
        return 0

    lax.fori_loop(0, ROUNDS - 1, round_of, 0)

    ready(ROUNDS - 1)

    def total_one(t, _):
        turn[pl.ds(t, 1), :] = jnp.sum(sums[t], axis=0, keepdims=True)
        return 0

    lax.fori_loop(0, 32, total_one, 0)

    def pack_sums(tile, _):
        r = first_block(tile)
        packed = spread(turn[pl.ds(r, 1), :])
        for s in range(4):
            packed = jnp.where(sub == s + 1, spread(turn[pl.ds(lax.rem(r + offset + s, 32), 1), :]), packed)
        for c in range(2):
            acc[tile, c, 16] = packed
        return 0

    lax.fori_loop(0, TILES, pack_sums, 0)

    def core_copy(i):
        _, tile = tile_at(i)
        return pltpu.make_async_remote_copy(
            src_ref=acc.at[tile, 1 - core],
            dst_ref=core_in.at[tile],
            send_sem=c_send.at[i],
            recv_sem=c_recv.at[i],
            device_id=other_core,
            device_id_type=MESH,
        )

    def plane_copy(i):
        e, tile = tile_at(i)
        return pltpu.make_async_remote_copy(
            src_ref=acc.at[tile, core],
            dst_ref=plane_in.at[i],
            send_sem=p_send.at[i],
            recv_sem=p_recv.at[i],
            device_id=plane_peer(e),
            device_id_type=MESH,
        )

    def join_cores(i):
        _, tile = tile_at(i)
        core_copy(i).wait_recv()
        for a in range(17):
            acc[tile, core, a] = acc[tile, core, a] + core_in[tile, a]

    def last_two(i, _):
        work(2 * i, roll_a, roll_b)
        core_copy(2 * i).start()
        work(2 * i + 1, roll_b, roll_a)
        core_copy(2 * i + 1).start()

        @pl.when(i > 0)
        def _():
            for k in (2 * i - 2, 2 * i - 1):
                join_cores(k)
                plane_copy(k).start()

        return 0

    lax.fori_loop(0, TILES // 2, last_two, 0)
    join_cores(TILES - 2)
    plane_copy(TILES - 2).start()
    join_cores(TILES - 1)

    own = z * 4 + x
    whole = [acc[own, core, a] for a in range(17)]
    for i in range(TILES - 1):
        plane_copy(i).wait_recv()
        for a in range(17):
            whole[a] = whole[a] + plane_in[i, a]
    for half in range(2):
        for a in range(8):
            column_out[half, a] = whole[half * 8 + a]
        column_out[half, 8] = whole[16]

    def column_copy(d):
        y = lax.rem(column + d, 4)
        return pltpu.make_async_remote_copy(
            src_ref=column_out.at[lax.rem(y, 2)],
            dst_ref=column_in.at[d - 1],
            send_sem=y_send.at[d - 1],
            recv_sem=y_recv.at[d - 1],
            device_id=column_peer(d),
            device_id_type=MESH,
        )

    for d in (2, 1, 3):
        column_copy(d).start()
    whole = [column_out[yl, a] for a in range(9)]
    for d in (1, 3, 2):
        column_copy(d).wait_recv()
        for a in range(9):
            whole[a] = whole[a] + column_in[d - 1, a]

    turn[pl.ds(0, 8), :] = whole[8]
    mine = spread(turn[pl.ds(0, 1), :])
    own_sums = [take(mine, row_index[q]) for q in range(2)]
    group = yl * 2 + core
    for s in range(4):
        theirs = take(spread(turn[pl.ds(1 + s, 1), :]), lane_h * 64 + group * 16 + lane_c)
        for q in range(2):
            metric = 2.0 * whole[s * 2 + q] / (own_sums[q] + theirs)
            undo = ((lane_c - (sub + 8 * q)) % 16) * 8 + lane % 8
            xin[pl.ds((s * 2 + q) * 8, 8), pl.ds(0, 128)] = take(metric, undo)
    flat = xin[:, pl.ds(0, 128)]
    turned = jnp.concatenate([flat, flat], axis=0).T
    for i in range(16):
        index = (lane // 16) * 16 + (i - lane % 16) % 16
        turn[pl.ds(i * 8, 8), :] = take(turned[i * 8 : i * 8 + 8, :], index)
    for rho in range(4):
        out[pl.ds(rho * 16, 16), :] = turn[pl.ds(rho * 2 + yh, 16, stride=8), :]

    def finish(i, _):
        core_copy(i).wait_send()
        return 0

    lax.fori_loop(0, TILES, finish, 0)

    def finish_plane(i, _):
        plane_copy(i).wait_send()
        return 0

    lax.fori_loop(0, TILES - 1, finish_plane, 0)

    def finish_round(j, _):
        def finish_one(i, _):
            a_copy(j, lax.rem(i * 13, 32)).wait_send()
            return 0

        lax.fori_loop(1, 32, finish_one, 0)
        return 0

    lax.fori_loop(0, ROUNDS, finish_round, 0)
    for d in (1, 2, 3):
        column_copy(d).wait_send()


def per_device(vectors, section):
    f32 = jnp.float32
    dma = pltpu.SemaphoreType.DMA
    flat = pl.pallas_call(
        kernel,
        out_shape=jax.ShapeDtypeStruct((64, 128), f32),
        in_specs=[pl.BlockSpec(memory_space=pltpu.SMEM), pl.BlockSpec(memory_space=pl.ANY)],
        out_specs=pl.BlockSpec(memory_space=pltpu.VMEM),
        scratch_shapes=[
            pltpu.VMEM((64, 8192), f32),
            pltpu.VMEM((32, 128, 128), f32),
            pltpu.VMEM((32, 128, 128), f32),
            pltpu.VMEM((32, NF, 128), f32),
            pltpu.VMEM((32, 4 * PITCH, 128), f32),
            pltpu.VMEM((NF, 2, 8, 128), f32),
            pltpu.VMEM((NF, 2, 8, 128), f32),
            pltpu.VMEM((TILES, 2, 17, 8, 128), f32),
            pltpu.VMEM((32, 8, 128), f32),
            pltpu.VMEM((TILES, 17, 8, 128), f32),
            pltpu.VMEM((TILES, 17, 8, 128), f32),
            pltpu.VMEM((2, 9, 8, 128), f32),
            pltpu.VMEM((3, 9, 8, 128), f32),
            pltpu.VMEM((128, 128), f32),
            dma((8,)),
            dma((ROUNDS, 32)),
            dma((ROUNDS, 32)),
            dma((TILES,)),
            dma((TILES,)),
            dma((TILES,)),
            dma((TILES,)),
            dma((3,)),
            dma((3,)),
        ],
        compiler_params=pltpu.CompilerParams(
            collective_id=0, has_side_effects=True, vmem_limit_bytes=48 * 2**20
        ),
    )(section, vectors)
    return flat[:, :64].reshape(64, 4, 16)


def solution(mesh):
    torus = Mesh(mesh.devices.reshape(4, 2, 4, 2, 2), AXES)
    placed = (P(("z", "yh", "x"), ("yl", "core")), P())
    return jax.shard_map(
        per_device,
        mesh=torus,
        in_specs=placed,
        out_specs=P(("z", "yh", "x"), None, ("yl", "core")),
        check_vma=False,
    )
```

profile of v0, /device:TPU:0, one launch (start us, length us, event | category | flops | bytes accessed | tf_op | source)
XLA Modules:
  0.0 121.7 jit_solution(15242516075070424639)
XLA Ops:
  0.7 0.0 copy-start
  0.7 1.6 %copy-done = f32[64,8192]{1,0:T(8,128)S(1)} copy-done((f32[64,8192]{1,0:T(8,128)S(1)}, f32[64,8192]{1,0:T(8,128)}, u32[]{:S(2)}) %copy-start) | copy-done | bytes 2097176
  2.2 118.7 %shard_map.28 = f32[64,128]{1,0:T(8,128)S(1)} custom-call(s32[1]{0:T(128)S(6)} %copy.5.section, f32[64,8192]{1,0:T(8,128)S(1)} %copy-done), custom_call_target="tpu_custom_call" | custom-call | tf_op jit(solution)/shard_map/pallas_call | solution.py:335
  121.0 0.7 copy.4
Async XLA Ops:
  0.7 1.6 %copy-start = (f32[64,8192]{1,0:T(8,128)S(1)}, f32[64,8192]{1,0:T(8,128)}, u32[]{:S(2)}) copy-start(f32[64,8192]{1,0:T(8,128)} %x_hbm.1) | copy-start | bytes 6291460
where the time goes:
time: 122 us
  Pallas kernels  119 us (98%)
  local copies, waits for them, and re-layouts  2.28 us (2%)
    pallas_call x1, Pallas kernels, per_device(): pl.pallas_call(kernel, out_shape=jax.ShapeDtypeStruct((64, 128), f32), in...  119 us

commit v1 on v0

v1 whole, which is shorter than its diff:
```python
import jax
import jax.numpy as jnp
from jax import lax
from jax.experimental import pallas as pl
from jax.experimental.pallas import tpu as pltpu
from jax.sharding import Mesh
from jax.sharding import PartitionSpec as P

MESH = pl.DeviceIdType.MESH
AXES = ("z", "yh", "x", "yl", "core")
FIELDS = (32, 64, 64, 96)
ROUNDS = len(FIELDS)
START = [sum(FIELDS[:j]) // 2 for j in range(ROUNDS)]
MOST = max(FIELDS)
TILES = 16
VREG = (8, 128)


def iota(axis):
    return lax.broadcasted_iota(jnp.int32, VREG, axis)


def spread(row):
    return jnp.broadcast_to(row, VREG)


def take(value, index):
    return jnp.take_along_axis(value, index, axis=1)


def kernel(
    section, x_hbm, out, xin, sent, got, places, high, low, rows, cols, roll_a, roll_b, acc, sums, core_in, plane_in, column_out, column_in,
    turn, flat_out, load_sem, a_send, a_recv, c_send, c_recv, p_send, p_recv, y_send, y_recv,
):
    z, yh, x, yl, core = (lax.axis_index(name) for name in AXES)
    offset = section[0]
    block = z * 8 + yh * 4 + x
    column = yh * 2 + yl

    def blk_peer(e):
        return (lax.rem(z + e // 8, 4), lax.rem(yh + (e // 4) % 2, 2), lax.rem(x + e % 4, 4), yl, core)

    def plane_peer(e):
        return (lax.rem(z + e // 4, 4), yh, lax.rem(x + e % 4, 4), yl, core)

    def column_peer(d):
        y = lax.rem(column + d, 4)
        return (z, y // 2, x, lax.rem(y, 2), core)

    other_core = (z, yh, x, yl, 1 - core)

    loads = []
    for i in range(8):
        part = pl.ds(i * 1024, 1024)
        loads.append(pltpu.make_async_copy(x_hbm.at[:, part], xin.at[:, part], load_sem.at[i]))
        loads[-1].start()

    barrier = pltpu.get_barrier_semaphore()
    for e in range(1, 32):
        pl.semaphore_signal(barrier, inc=1, device_id=blk_peer(e), device_id_type=MESH)
    for peer in (column_peer(1), column_peer(3), other_core):
        pl.semaphore_signal(barrier, inc=1, device_id=peer, device_id_type=MESH)

    lane, sub = iota(1), iota(0)
    lane_c = lane // 8

    with jax.named_scope("load_wait"):
        for load in loads:
            load.wait()

    def transpose_some(n, _):
        for k in range(8):
            u = n * 8 + k
            left = xin[:, pl.ds(pl.multiple_of(u * 128, 128), 128)]
            right = xin[:, pl.ds(pl.multiple_of(u * 128 + 4096, 128), 128)]
            sent[u] = jnp.concatenate([left, right], axis=0).T
        return 0

    with jax.named_scope("transpose"):
        lax.fori_loop(0, 4, transpose_some, 0)
        got[block] = sent[block]
    for tile in range(32):
        sums[tile] = jnp.zeros(VREG, jnp.float32)

    def clear(tile, _):
        for c in range(2):
            for a in range(16):
                acc[tile, c, a] = jnp.zeros(VREG, jnp.float32)
        return 0

    with jax.named_scope("clear"):
        lax.fori_loop(0, TILES, clear, 0)
    with jax.named_scope("barrier"):
        pl.semaphore_wait(barrier, 34)

    def a_copy(j, e):
        z2, yh2, x2, _, _ = blk_peer(e)
        part = pl.ds(START[j], FIELDS[j] // 2)
        return pltpu.make_async_remote_copy(
            src_ref=sent.at[z2 * 8 + yh2 * 4 + x2, part],
            dst_ref=got.at[block, part],
            send_sem=a_send.at[j, e],
            recv_sem=a_recv.at[j, e],
            device_id=blk_peer(e),
            device_id_type=MESH,
        )

    def over_peers(act):
        def one(i, _):
            act(lax.rem(i * 13, 32))
            return 0

        lax.fori_loop(1, 32, one, 0)

    with jax.named_scope("send"):
        for j in range(ROUNDS):
            over_peers(lambda e: a_copy(j, e).start())

    def tile_at(i):
        e = lax.rem((15 - i) * 7, 16)
        return e, lax.rem(z + e // 4, 4) * 4 + lax.rem(x + e % 4, 4)

    def first_block(tile):
        return (tile // 4) * 8 + lax.rem(tile, 4)

    def place():
        here = lax.broadcasted_iota(jnp.int32, (256, 128), 0)
        to = lax.broadcasted_iota(jnp.int32, (256, 128), 1)
        for order in range(5):
            group = (to // 2) % 4 if order == 0 else order - 1
            for h in range(2):
                origin = (to % 2) * 128 + h * 64 + group * 16 + to // 8
                part = pl.ds((order * 2 + h) * 128, 128)
                places[:, part] = jnp.where(here == origin, 1.0, 0.0).astype(jnp.bfloat16)

    def arrange(j):
        half = FIELDS[j] // 2
        pitch = FIELDS[j] + 8
        n = {16: 32, 32: 32, 48: 16}[half]

        def split(b, _):
            for k in range(4):
                t = b * 4 + k
                here = pl.ds(pl.multiple_of(t * half, 16), half)
                for i, source in enumerate((t, lax.rem(t + 4, 32))):
                    value = got[source, pl.ds(START[j], half), :]
                    top = value.astype(jnp.bfloat16)
                    high[here, pl.ds(i * 128, 128)] = top
                    low[here, pl.ds(i * 128, 128)] = (value - top.astype(jnp.float32)).astype(jnp.bfloat16)
            return 0

        def spread_out(b, _):
            here = pl.ds(pl.multiple_of(b * n * half, 16), n * half)
            for order in range(5):
                weight = places[:, pl.ds(order * 256, 256)]
                value = jnp.dot(high[here, :], weight, preferred_element_type=jnp.float32)
                value = value + jnp.dot(low[here, :], weight, preferred_element_type=jnp.float32)
                for k in range(n):
                    for h in range(2):
                        part = value[k * half : (k + 1) * half, h * 128 : h * 128 + 128]
                        if order == 0:
                            rows[b * n + k, pl.ds(h * half, half), :] = part
                        else:
                            cols[b * n + k, pl.ds((order - 1) * pitch + h * half, half), :] = part
            return 0

        def add_up(b, _):
            for k in range(4):
                total = sums[b * 4 + k]
                for o in range(FIELDS[j] // 8):
                    total = total + rows[b * 4 + k, pl.ds(o * 8, 8), :]
                sums[b * 4 + k] = total
            return 0

        lax.fori_loop(0, 8, split, 0)
        lax.fori_loop(0, 32 // n, spread_out, 0)
        lax.fori_loop(0, 8, add_up, 0)

    def turn_field(j, target, r, f):
        row = spread(rows[r, pl.ds(f, 1), :])
        for q in range(2):
            target[f, q] = pltpu.roll(row, 64 * q, 1, stride=8, stride_axis=0)

    def work(j, i, now, later):
        _, tile = tile_at(i)
        r = first_block(tile)
        follow = first_block(tile_at(lax.rem(i + 1, TILES))[1])
        partner = [lax.rem(r + offset + s, 32) for s in range(4)]
        total = [acc[tile, a // 16, a % 16] for a in range(32)]
        for f in range(FIELDS[j]):
            turned = [now[f, q] for q in range(2)]
            for s in range(4):
                for g in range(4):
                    other = spread(cols[partner[s], pl.ds(g * (FIELDS[j] + 8) + f, 1), :])
                    for q in range(2):
                        a = (g % 2) * 16 + (g // 2) * 8 + s * 2 + q
                        total[a] = total[a] + jnp.minimum(turned[q], other)
            turn_field(j, later, follow, f)
        for a in range(32):
            acc[tile, a // 16, a % 16] = total[a]

    def first_turn(j):
        r0 = first_block(tile_at(0)[1])

        def some(b, _):
            for f in range(16):
                turn_field(j, roll_a, r0, b * 16 + f)
            return 0

        with jax.named_scope("first"):
            lax.fori_loop(0, FIELDS[j] // 16, some, 0)

    def arrived(j):
        with jax.named_scope("got_wait"):
            over_peers(lambda e: a_copy(j, e).wait_recv())

    def ready(j):
        arrived(j)
        with jax.named_scope("arrange"):
            arrange(j)
        first_turn(j)

    def round_of(j):
        ready(j)

        def two(i, _):
            work(j, 2 * i, roll_a, roll_b)

            @pl.when(i < TILES)
            def _():
                work(j, 2 * i + 1, roll_b, roll_a)

            return 0

        with jax.named_scope("work"):
            lax.fori_loop(0, TILES // 2, two, 0)

    with jax.named_scope("place"):
        place()
    for j in range(ROUNDS - 1):
        round_of(j)
    ready(ROUNDS - 1)

    def total_one(t, _):
        turn[pl.ds(t, 1), :] = jnp.sum(sums[t], axis=0, keepdims=True)
        return 0

    with jax.named_scope("total"):
        lax.fori_loop(0, 32, total_one, 0)

    def pack_sums(tile, _):
        r = first_block(tile)
        packed = spread(turn[pl.ds(r, 1), :])
        for s in range(4):
            packed = jnp.where(sub == s + 1, spread(turn[pl.ds(lax.rem(r + offset + s, 32), 1), :]), packed)
        for c in range(2):
            acc[tile, c, 16] = packed
        return 0

    with jax.named_scope("pack"):
        lax.fori_loop(0, TILES, pack_sums, 0)

    def core_copy(i):
        _, tile = tile_at(i)
        return pltpu.make_async_remote_copy(
            src_ref=acc.at[tile, 1 - core],
            dst_ref=core_in.at[tile],
            send_sem=c_send.at[i],
            recv_sem=c_recv.at[i],
            device_id=other_core,
            device_id_type=MESH,
        )

    def plane_copy(i):
        e, tile = tile_at(i)
        return pltpu.make_async_remote_copy(
            src_ref=acc.at[tile, core],
            dst_ref=plane_in.at[i],
            send_sem=p_send.at[i],
            recv_sem=p_recv.at[i],
            device_id=plane_peer(e),
            device_id_type=MESH,
        )

    def join_cores(i):
        _, tile = tile_at(i)
        core_copy(i).wait_recv()
        for a in range(17):
            acc[tile, core, a] = acc[tile, core, a] + core_in[tile, a]

    def last_two(i, _):
        work(ROUNDS - 1, 2 * i, roll_a, roll_b)
        core_copy(2 * i).start()
        work(ROUNDS - 1, 2 * i + 1, roll_b, roll_a)
        core_copy(2 * i + 1).start()

        @pl.when(i > 0)
        def _():
            for k in (2 * i - 2, 2 * i - 1):
                join_cores(k)
                plane_copy(k).start()

        return 0

    with jax.named_scope("last_work"):
        lax.fori_loop(0, TILES // 2, last_two, 0)
    with jax.named_scope("last_join"):
        join_cores(TILES - 2)
        plane_copy(TILES - 2).start()
        join_cores(TILES - 1)

    with jax.named_scope("finish"):
        for j in range(ROUNDS):
            over_peers(lambda e: a_copy(j, e).wait_send())
    own = z * 4 + x
    whole = [acc[own, core, a] for a in range(17)]
    for i in range(TILES - 1):
        with jax.named_scope("plane_wait"):
            plane_copy(i).wait_recv()
        for a in range(17):
            whole[a] = whole[a] + plane_in[i, a]
    for half in range(2):
        for a in range(8):
            column_out[half, a] = whole[half * 8 + a]
        column_out[half, 8] = whole[16]

    def column_copy(d):
        y = lax.rem(column + d, 4)
        return pltpu.make_async_remote_copy(
            src_ref=column_out.at[lax.rem(y, 2)],
            dst_ref=column_in.at[d - 1],
            send_sem=y_send.at[d - 1],
            recv_sem=y_recv.at[d - 1],
            device_id=column_peer(d),
            device_id_type=MESH,
        )

    for d in (2, 1, 3):
        column_copy(d).start()

    def finish(i, _):
        core_copy(i).wait_send()
        return 0

    def finish_plane(i, _):
        plane_copy(i).wait_send()
        return 0

    lax.fori_loop(0, TILES, finish, 0)
    lax.fori_loop(0, TILES - 1, finish_plane, 0)
    whole = [column_out[yl, a] for a in range(9)]
    for d in (1, 3, 2):
        with jax.named_scope("column_wait"):
            column_copy(d).wait_recv()
        column_copy(d).wait_send()
        for a in range(9):
            whole[a] = whole[a] + column_in[d - 1, a]

    with jax.named_scope("end"):
        turn[pl.ds(0, 8), :] = whole[8]
        mine = spread(turn[pl.ds(0, 1), :])
        pick = lane_c * 8 + (yl * 2 + core) * 2 + lane % 2
        theirs = [take(spread(turn[pl.ds(1 + s, 1), :]), pick) for s in range(4)]
        for q in range(2):
            own_sums = pltpu.roll(mine, 64 * q, 1, stride=8, stride_axis=0)
            undo = ((lane_c + sub + 8 * q) % 16) * 8 + lane % 8
            for s in range(4):
                metric = 2.0 * whole[s * 2 + q] / (own_sums + theirs[s])
                flat_out[pl.ds(q * 32 + s, 8, stride=4), :] = take(metric, undo)
        flat = flat_out[...]
        turned = jnp.concatenate([flat, flat], axis=0).T
        for i in range(16):
            part = turned[i * 8 : i * 8 + 8, :]
            turn[pl.ds(i * 8, 8), :] = pltpu.roll(part, 4 * i, 1) if i else part
        swap = (lane % 16) * 4 + lane // 16
        for i in range(8):
            part = turn[pl.ds((i % 2) * 64 + (i // 2) * 2 + yh, 8, stride=8), :]
            out[pl.ds(i * 8, 8), :] = take(part, swap % 128)


def per_device(vectors, section):
    f32 = jnp.float32
    dma = pltpu.SemaphoreType.DMA
    flat = pl.pallas_call(
        kernel,
        out_shape=jax.ShapeDtypeStruct((64, 128), f32),
        in_specs=[pl.BlockSpec(memory_space=pltpu.SMEM), pl.BlockSpec(memory_space=pl.ANY)],
        out_specs=pl.BlockSpec(memory_space=pltpu.VMEM),
        scratch_shapes=[
            pltpu.VMEM((64, 8192), f32),
            pltpu.VMEM((32, 128, 128), f32),
            pltpu.VMEM((32, 128, 128), f32),
            pltpu.VMEM((256, 1280), jnp.bfloat16),
            pltpu.VMEM((16 * MOST, 256), jnp.bfloat16),
            pltpu.VMEM((16 * MOST, 256), jnp.bfloat16),
            pltpu.VMEM((32, MOST, 128), f32),
            pltpu.VMEM((32, 4 * (MOST + 8), 128), f32),
            pltpu.VMEM((MOST, 2, 8, 128), f32),
            pltpu.VMEM((MOST, 2, 8, 128), f32),
            pltpu.VMEM((TILES, 2, 17, 8, 128), f32),
            pltpu.VMEM((32, 8, 128), f32),
            pltpu.VMEM((TILES, 17, 8, 128), f32),
            pltpu.VMEM((TILES, 17, 8, 128), f32),
            pltpu.VMEM((2, 9, 8, 128), f32),
            pltpu.VMEM((3, 9, 8, 128), f32),
            pltpu.VMEM((128, 128), f32),
            pltpu.VMEM((64, 128), f32),
            dma((8,)),
            dma((ROUNDS, 32)),
            dma((ROUNDS, 32)),
            dma((TILES,)),
            dma((TILES,)),
            dma((TILES,)),
            dma((TILES,)),
            dma((3,)),
            dma((3,)),
        ],
        compiler_params=pltpu.CompilerParams(
            collective_id=0, has_side_effects=True, vmem_limit_bytes=63 * 2**20
        ),
    )(section, vectors)
    return flat[:, :64].reshape(64, 4, 16)


def solution(mesh):
    torus = Mesh(mesh.devices.reshape(4, 2, 4, 2, 2), AXES)
    placed = (P(("z", "yh", "x"), ("yl", "core")), P())
    return jax.shard_map(
        per_device,
        mesh=torus,
        in_specs=placed,
        out_specs=P(("z", "yh", "x"), None, ("yl", "core")),
        check_vma=False,
    )
```

time: 122 us -> 85.7 us (0.70)
  Pallas kernels: 119 us -> 83.4 us
    pallas_call x1, Pallas kernels: 119 us -> 83.4 us  [per_device(): pl.pallas_call(kernel, out_shape=jax.ShapeDtypeStruct((64, 128), f32), in...]
    unnamed x2 -> x0, local copies, waits for them, and re-layouts: 1.58 us -> none
where the time goes in v1:
time: 85.7 us; the launch traced here: 85.5 us
  Pallas kernels  83.4 us (97%)
  local copies, waits for them, and re-layouts  1.46 us (2%)
    pallas_call x1, Pallas kernels, per_device(): pl.pallas_call(kernel, out_shape=jax.ShapeDtypeStruct((64, 128), f32), in...  83.4 us

profile of v1, /device:TPU:0, one launch (start us, length us, event | category | flops | bytes accessed | tf_op | source)
XLA Modules:
  0.0 85.5 jit_solution(7684496419773318422)
XLA Ops:
  0.7 83.4 %shard_map.28 = f32[64,128]{1,0:T(8,128)} custom-call(s32[1]{0:T(128)S(6)} %copy.5.section, f32[64,8192]{1,0:T(8,128)} %x_hbm.1), custom_call_target="tpu_custom_call" | custom-call | tf_op jit(solution)/shard_map/pallas_call | solution.py:384
  84.0 1.5 %copy.4 = f32[64,64]{0,1:T(8,128)} copy(f32[64,64]{1,0:T(8,128)} %bitcast.2) | data formatting | bytes 32768 | tf_op jit(solution)/shard_map/slice | solution.py:422

commit v2 on v1

--- a/solution.py
+++ b/solution.py
@@ -7,12 +7,20 @@
 from jax.sharding import PartitionSpec as P
 
 MESH = pl.DeviceIdType.MESH
+
+
+def hops(e):
+    return min(e // 8, 4 - e // 8) + 2 * ((e // 4) % 2) + min(e % 4, 4 - e % 4)
+
+
+FAR_FIRST = sorted(range(1, 32), key=lambda e: (-hops(e), (e * 13) % 32))
 AXES = ("z", "yh", "x", "yl", "core")
-FIELDS = (32, 64, 64, 96)
+FIELDS = (32, 64, 32, 128)
 ROUNDS = len(FIELDS)
 START = [sum(FIELDS[:j]) // 2 for j in range(ROUNDS)]
 MOST = max(FIELDS)
 TILES = 16
+ORDER = (10, 9, 11, 6, 14, 5, 7, 13, 15, 2, 8, 1, 12, 3, 4, 0)
 VREG = (8, 128)
 
 
@@ -52,11 +60,11 @@
     loads = []
     for i in range(8):
         part = pl.ds(i * 1024, 1024)
-        loads.append(pltpu.make_async_copy(x_hbm.at[:, part], xin.at[:, part], load_sem.at[i]))
+        loads.append(pltpu.make_async_copy(x_hbm.at[:, part], xin.at[:, part], load_sem))
         loads[-1].start()
 
     barrier = pltpu.get_barrier_semaphore()
-    for e in range(1, 32):
+    for e in FAR_FIRST:
         pl.semaphore_signal(barrier, inc=1, device_id=blk_peer(e), device_id_type=MESH)
     for peer in (column_peer(1), column_peer(3), other_core):
         pl.semaphore_signal(barrier, inc=1, device_id=peer, device_id_type=MESH)
@@ -65,8 +73,7 @@
     lane_c = lane // 8
 
     with jax.named_scope("load_wait"):
-        for load in loads:
-            load.wait()
+        pltpu.make_async_copy(x_hbm, xin, load_sem).wait()
 
     def transpose_some(n, _):
         for k in range(8):
@@ -88,8 +95,6 @@
                 acc[tile, c, a] = jnp.zeros(VREG, jnp.float32)
         return 0
 
-    with jax.named_scope("clear"):
-        lax.fori_loop(0, TILES, clear, 0)
     with jax.named_scope("barrier"):
         pl.semaphore_wait(barrier, 34)
 
@@ -99,8 +104,8 @@
         return pltpu.make_async_remote_copy(
             src_ref=sent.at[z2 * 8 + yh2 * 4 + x2, part],
             dst_ref=got.at[block, part],
-            send_sem=a_send.at[j, e],
-            recv_sem=a_recv.at[j, e],
+            send_sem=a_send,
+            recv_sem=a_recv.at[j],
             device_id=blk_peer(e),
             device_id_type=MESH,
         )
@@ -113,11 +118,13 @@
         lax.fori_loop(1, 32, one, 0)
 
     with jax.named_scope("send"):
-        for j in range(ROUNDS):
+        for e in FAR_FIRST:
+            a_copy(0, e).start()
+        for j in range(1, ROUNDS):
             over_peers(lambda e: a_copy(j, e).start())
 
-    def tile_at(i):
-        e = lax.rem((15 - i) * 7, 16)
+    def tile_at(i, last=True):
+        e = sum(jnp.where(i == k, ORDER[k], 0) for k in range(TILES)) if last else i
         return e, lax.rem(z + e // 4, 4) * 4 + lax.rem(x + e % 4, 4)
 
     def first_block(tile):
@@ -136,17 +143,22 @@
     def arrange(j):
         half = FIELDS[j] // 2
         pitch = FIELDS[j] + 8
-        n = {16: 32, 32: 32, 48: 16}[half]
+        n = min(32, 1024 // half)
 
         def split(b, _):
-            for k in range(4):
-                t = b * 4 + k
-                here = pl.ds(pl.multiple_of(t * half, 16), half)
-                for i, source in enumerate((t, lax.rem(t + 4, 32))):
-                    value = got[source, pl.ds(START[j], half), :]
-                    top = value.astype(jnp.bfloat16)
+            for k in range(8):
+                t = b * 8 + k
+                value = got[t, pl.ds(START[j], half), :]
+                top = value.astype(jnp.bfloat16)
+                rest = (value - top.astype(jnp.float32)).astype(jnp.bfloat16)
+                for i, target in enumerate((t, lax.rem(t + 28, 32))):
+                    here = pl.ds(pl.multiple_of(target * half, 16), half)
                     high[here, pl.ds(i * 128, 128)] = top
-                    low[here, pl.ds(i * 128, 128)] = (value - top.astype(jnp.float32)).astype(jnp.bfloat16)
+                    low[here, pl.ds(i * 128, 128)] = rest
+                total = sums[t]
+                for o in range(half // 8):
+                    total = total + value[o * 8 : o * 8 + 8]
+                sums[t] = total
             return 0
 
         def spread_out(b, _):
@@ -164,17 +176,8 @@
                             cols[b * n + k, pl.ds((order - 1) * pitch + h * half, half), :] = part
             return 0
 
-        def add_up(b, _):
-            for k in range(4):
-                total = sums[b * 4 + k]
-                for o in range(FIELDS[j] // 8):
-                    total = total + rows[b * 4 + k, pl.ds(o * 8, 8), :]
-                sums[b * 4 + k] = total
-            return 0
-
-        lax.fori_loop(0, 8, split, 0)
+        lax.fori_loop(0, 4, split, 0)
         lax.fori_loop(0, 32 // n, spread_out, 0)
-        lax.fori_loop(0, 8, add_up, 0)
 
     def turn_field(j, target, r, f):
         row = spread(rows[r, pl.ds(f, 1), :])
@@ -182,9 +185,10 @@
             target[f, q] = pltpu.roll(row, 64 * q, 1, stride=8, stride_axis=0)
 
     def work(j, i, now, later):
-        _, tile = tile_at(i)
+        last = j == ROUNDS - 1
+        _, tile = tile_at(i, last)
         r = first_block(tile)
-        follow = first_block(tile_at(lax.rem(i + 1, TILES))[1])
+        follow = first_block(tile_at(lax.rem(i + 1, TILES), last)[1])
         partner = [lax.rem(r + offset + s, 32) for s in range(4)]
         total = [acc[tile, a // 16, a % 16] for a in range(32)]
         for f in range(FIELDS[j]):
@@ -200,19 +204,20 @@
             acc[tile, a // 16, a % 16] = total[a]
 
     def first_turn(j):
-        r0 = first_block(tile_at(0)[1])
+        r0 = first_block(tile_at(0, j == ROUNDS - 1)[1])
 
         def some(b, _):
-            for f in range(16):
-                turn_field(j, roll_a, r0, b * 16 + f)
+            for f in range(32):
+                turn_field(j, roll_a, r0, b * 32 + f)
             return 0
 
         with jax.named_scope("first"):
-            lax.fori_loop(0, FIELDS[j] // 16, some, 0)
+            lax.fori_loop(0, FIELDS[j] // 32, some, 0)
 
     def arrived(j):
         with jax.named_scope("got_wait"):
-            over_peers(lambda e: a_copy(j, e).wait_recv())
+            part = pl.ds(START[j], FIELDS[j] // 2)
+            pltpu.make_async_copy(sent.at[pl.ds(0, 31), part], got.at[pl.ds(0, 31), part], a_recv.at[j]).wait()
 
     def ready(j):
         arrived(j)
@@ -237,16 +242,26 @@
 
     with jax.named_scope("place"):
         place()
+        lax.fori_loop(0, TILES, clear, 0)
     for j in range(ROUNDS - 1):
         round_of(j)
     ready(ROUNDS - 1)
 
-    def total_one(t, _):
-        turn[pl.ds(t, 1), :] = jnp.sum(sums[t], axis=0, keepdims=True)
+    def total_one(b, _):
+        for k in range(8):
+            turn[pl.ds(b * 8 + k, 1), :] = jnp.sum(sums[b * 8 + k], axis=0, keepdims=True)
         return 0
 
     with jax.named_scope("total"):
-        lax.fori_loop(0, 32, total_one, 0)
+        lax.fori_loop(0, 4, total_one, 0)
+        natural = turn[pl.ds(0, 32), :]
+        natural = jnp.concatenate([natural, jnp.concatenate([natural[4:], natural[:4]], axis=0)], axis=1)
+        top = natural.astype(jnp.bfloat16)
+        rest = (natural - top.astype(jnp.float32)).astype(jnp.bfloat16)
+        weight = places[:, pl.ds(0, 256)]
+        both = jnp.dot(top, weight, preferred_element_type=jnp.float32)
+        both = both + jnp.dot(rest, weight, preferred_element_type=jnp.float32)
+        turn[pl.ds(0, 32), :] = both[:, :128] + both[:, 128:]
 
     def pack_sums(tile, _):
         r = first_block(tile)
@@ -265,7 +280,7 @@
         return pltpu.make_async_remote_copy(
             src_ref=acc.at[tile, 1 - core],
             dst_ref=core_in.at[tile],
-            send_sem=c_send.at[i],
+            send_sem=c_send,
             recv_sem=c_recv.at[i],
             device_id=other_core,
             device_id_type=MESH,
@@ -276,8 +291,8 @@
         return pltpu.make_async_remote_copy(
             src_ref=acc.at[tile, core],
             dst_ref=plane_in.at[i],
-            send_sem=p_send.at[i],
-            recv_sem=p_recv.at[i],
+            send_sem=p_send,
+            recv_sem=p_recv,
             device_id=plane_peer(e),
             device_id_type=MESH,
         )
@@ -310,13 +325,12 @@
         join_cores(TILES - 1)
 
     with jax.named_scope("finish"):
-        for j in range(ROUNDS):
-            over_peers(lambda e: a_copy(j, e).wait_send())
+        pltpu.make_async_copy(got.at[pl.ds(0, 31)], sent.at[pl.ds(0, 31)], a_send).wait()
     own = z * 4 + x
     whole = [acc[own, core, a] for a in range(17)]
+    with jax.named_scope("plane_wait"):
+        pltpu.make_async_copy(acc.at[pl.ds(0, 15), 0], plane_in.at[pl.ds(0, 15)], p_recv).wait()
     for i in range(TILES - 1):
-        with jax.named_scope("plane_wait"):
-            plane_copy(i).wait_recv()
         for a in range(17):
             whole[a] = whole[a] + plane_in[i, a]
     for half in range(2):
@@ -329,8 +343,8 @@
         return pltpu.make_async_remote_copy(
             src_ref=column_out.at[lax.rem(y, 2)],
             dst_ref=column_in.at[d - 1],
-            send_sem=y_send.at[d - 1],
-            recv_sem=y_recv.at[d - 1],
+            send_sem=y_send,
+            recv_sem=y_recv,
             device_id=column_peer(d),
             device_id_type=MESH,
         )
@@ -338,23 +352,15 @@
     for d in (2, 1, 3):
         column_copy(d).start()
 
-    def finish(i, _):
-        core_copy(i).wait_send()
-        return 0
-
-    def finish_plane(i, _):
-        plane_copy(i).wait_send()
-        return 0
-
-    lax.fori_loop(0, TILES, finish, 0)
-    lax.fori_loop(0, TILES - 1, finish_plane, 0)
+    pltpu.make_async_copy(acc.at[:, 0], core_in, c_send).wait()
+    pltpu.make_async_copy(acc.at[pl.ds(0, 15), 0], plane_in.at[pl.ds(0, 15)], p_send).wait()
     whole = [column_out[yl, a] for a in range(9)]
-    for d in (1, 3, 2):
-        with jax.named_scope("column_wait"):
-            column_copy(d).wait_recv()
-        column_copy(d).wait_send()
+    with jax.named_scope("column_wait"):
+        pltpu.make_async_copy(column_in, column_in, y_recv).wait()
+        pltpu.make_async_copy(column_in, column_in, y_send).wait()
+    for d in range(3):
         for a in range(9):
-            whole[a] = whole[a] + column_in[d - 1, a]
+            whole[a] = whole[a] + column_in[d, a]
 
     with jax.named_scope("end"):
         turn[pl.ds(0, 8), :] = whole[8]
@@ -367,15 +373,18 @@
             for s in range(4):
                 metric = 2.0 * whole[s * 2 + q] / (own_sums + theirs[s])
                 flat_out[pl.ds(q * 32 + s, 8, stride=4), :] = take(metric, undo)
-        flat = flat_out[...]
+        flat = flat_out[pl.ds(0, 64), :]
         turned = jnp.concatenate([flat, flat], axis=0).T
         for i in range(16):
             part = turned[i * 8 : i * 8 + 8, :]
             turn[pl.ds(i * 8, 8), :] = pltpu.roll(part, 4 * i, 1) if i else part
-        swap = (lane % 16) * 4 + lane // 16
         for i in range(8):
             part = turn[pl.ds((i % 2) * 64 + (i // 2) * 2 + yh, 8, stride=8), :]
-            out[pl.ds(i * 8, 8), :] = take(part, swap % 128)
+            flat_out[pl.ds(i * 8, 8), :] = part
+            flat_out[pl.ds(64 + i * 8, 8), :] = part
+        turn[...] = flat_out[...].T
+        for s in range(4):
+            out[pl.ds(s * 16, 16), :] = turn[pl.ds(s, 16, stride=4), :]
 
 
 def per_device(vectors, section):
@@ -404,22 +413,22 @@
             pltpu.VMEM((2, 9, 8, 128), f32),
             pltpu.VMEM((3, 9, 8, 128), f32),
             pltpu.VMEM((128, 128), f32),
-            pltpu.VMEM((64, 128), f32),
-            dma((8,)),
-            dma((ROUNDS, 32)),
-            dma((ROUNDS, 32)),
+            pltpu.VMEM((128, 128), f32),
+            dma,
+            dma,
+            dma((ROUNDS,)),
+            dma,
             dma((TILES,)),
-            dma((TILES,)),
-            dma((TILES,)),
-            dma((TILES,)),
-            dma((3,)),
-            dma((3,)),
+            dma,
+            dma,
+            dma,
+            dma,
         ],
         compiler_params=pltpu.CompilerParams(
             collective_id=0, has_side_effects=True, vmem_limit_bytes=63 * 2**20
         ),
     )(section, vectors)
-    return flat[:, :64].reshape(64, 4, 16)
+    return flat[:, :64].reshape(4, 16, 64).transpose(2, 0, 1)
 
 
 def solution(mesh):

time: 85.7 us -> 77.1 us (0.90)
  Pallas kernels: 83.4 us -> 74.8 us
    pallas_call x1, Pallas kernels: 83.4 us -> 74.8 us  [per_device(): pl.pallas_call(kernel, out_shape=jax.ShapeDtypeStruct((64, 128), f32), in...]
    slice x1 -> x0, local copies, waits for them, and re-layouts: 1.46 us -> none  [per_device(): return flat[:, :64].reshape(64, 4, 16)]
    unnamed x0 -> x1, local copies, waits for them, and re-layouts: none -> 1.38 us
where the time goes in v2:
time: 77.1 us; the launch traced here: 76.9 us
  Pallas kernels  74.8 us (97%)
  local copies, waits for them, and re-layouts  1.38 us (2%)
    pallas_call x1, Pallas kernels, per_device(): pl.pallas_call(kernel, out_shape=jax.ShapeDtypeStruct((64, 128), f32), in...  74.8 us

profile of v2, /device:TPU:0, one launch (start us, length us, event | category | flops | bytes accessed | tf_op | source)
XLA Modules:
  0.0 76.9 jit_solution(16975058696359493160)
XLA Ops:
  0.7 74.8 %shard_map.28 = f32[64,128]{1,0:T(8,128)} custom-call(s32[1]{0:T(128)S(6)} %copy.4.section, f32[64,8192]{1,0:T(8,128)} %x_hbm.1), custom_call_target="tpu_custom_call" | custom-call | tf_op jit(solution)/shard_map/pallas_call | solution.py:393
  75.5 1.4 %copy.5 = f32[64,4,16]{0,2,1:T(8,128)} copy(f32[64,4,16]{0,2,1:T(8,128)} %bitcast.4) | data formatting | bytes 32768

commit v3 on v2

--- a/solution.py
+++ b/solution.py
@@ -37,7 +37,7 @@
 
 
 def kernel(
-    section, x_hbm, out, xin, sent, got, places, high, low, rows, cols, roll_a, roll_b, acc, sums, core_in, plane_in, column_out, column_in,
+    section, x_hbm, out, xin, sent, got, places, near, cross, rows, cols, roll_a, roll_b, acc, sums, core_in, plane_in, column_out, column_in,
     turn, flat_out, load_sem, a_send, a_recv, c_send, c_recv, p_send, p_recv, y_send, y_recv,
 ):
     z, yh, x, yl, core = (lax.axis_index(name) for name in AXES)
@@ -78,8 +78,8 @@
     def transpose_some(n, _):
         for k in range(8):
             u = n * 8 + k
-            left = xin[:, pl.ds(pl.multiple_of(u * 128, 128), 128)]
-            right = xin[:, pl.ds(pl.multiple_of(u * 128 + 4096, 128), 128)]
+            left = xin[:, pl.ds(pl.multiple_of(u * 128 + yh * 4096, 128), 128)]
+            right = xin[:, pl.ds(pl.multiple_of(u * 128 + (1 - yh) * 4096, 128), 128)]
             sent[u] = jnp.concatenate([left, right], axis=0).T
         return 0
 
@@ -131,14 +131,21 @@
         return (tile // 4) * 8 + lax.rem(tile, 4)
 
     def place():
-        here = lax.broadcasted_iota(jnp.int32, (256, 128), 0)
+        here = lax.broadcasted_iota(jnp.int32, (256, 128), 0) % 128
         to = lax.broadcasted_iota(jnp.int32, (256, 128), 1)
         for order in range(5):
-            group = (to // 2) % 4 if order == 0 else order - 1
-            for h in range(2):
-                origin = (to % 2) * 128 + h * 64 + group * 16 + to // 8
-                part = pl.ds((order * 2 + h) * 128, 128)
-                places[:, part] = jnp.where(here == origin, 1.0, 0.0).astype(jnp.bfloat16)
+            group = (to // 2) % 4 if order == 4 else order
+            for side in range(2):
+                origin = ((to + side) % 2) * 64 + group * 16 + to // 8
+                places[side, :, pl.ds(order * 128, 128)] = jnp.where(here == origin, 1.0, 0.0).astype(jnp.bfloat16)
+
+    def parts(value):
+        top = value.astype(jnp.bfloat16)
+        return top, (value - top.astype(jnp.float32)).astype(jnp.bfloat16)
+
+    def sides(this, that):
+        left = lax.broadcasted_iota(jnp.int32, this.shape, 1) < 64
+        return jnp.where(left, this, that), jnp.where(left, that, this)
 
     def arrange(j):
         half = FIELDS[j] // 2
@@ -148,36 +155,41 @@
         def split(b, _):
             for k in range(8):
                 t = b * 8 + k
-                value = got[t, pl.ds(START[j], half), :]
-                top = value.astype(jnp.bfloat16)
-                rest = (value - top.astype(jnp.float32)).astype(jnp.bfloat16)
-                for i, target in enumerate((t, lax.rem(t + 28, 32))):
-                    here = pl.ds(pl.multiple_of(target * half, 16), half)
-                    high[here, pl.ds(i * 128, 128)] = top
-                    low[here, pl.ds(i * 128, 128)] = rest
+                here = pl.ds(pl.multiple_of(t * half, 16), half)
+                this = got[t, pl.ds(START[j], half), :]
+                for target, value in zip((near, cross), sides(this, got[lax.rem(t + 4, 32), pl.ds(START[j], half), :])):
+                    for i, part in enumerate(parts(value)):
+                        target[here, pl.ds(i * 128, 128)] = part
                 total = sums[t]
                 for o in range(half // 8):
-                    total = total + value[o * 8 : o * 8 + 8]
+                    total = total + this[o * 8 : o * 8 + 8]
                 sums[t] = total
             return 0
 
-        def spread_out(b, _):
+        def spread_cols(b, _):
             here = pl.ds(pl.multiple_of(b * n * half, 16), n * half)
-            for order in range(5):
-                weight = places[:, pl.ds(order * 256, 256)]
-                value = jnp.dot(high[here, :], weight, preferred_element_type=jnp.float32)
-                value = value + jnp.dot(low[here, :], weight, preferred_element_type=jnp.float32)
-                for k in range(n):
-                    for h in range(2):
-                        part = value[k * half : (k + 1) * half, h * 128 : h * 128 + 128]
-                        if order == 0:
-                            rows[b * n + k, pl.ds(h * half, half), :] = part
-                        else:
-                            cols[b * n + k, pl.ds((order - 1) * pitch + h * half, half), :] = part
+            for pair in range(2):
+                for side, source in enumerate((near, cross)):
+                    weight = places[side, :, pl.ds(pair * 256, 256)]
+                    value = jnp.dot(source[here, :], weight, preferred_element_type=jnp.float32)
+                    for k in range(n):
+                        at = ((k // 4 + side) % 2) * half
+                        for i in range(2):
+                            part = value[k * half : (k + 1) * half, i * 128 : i * 128 + 128]
+                            cols[b * n + k, pl.ds((pair * 2 + i) * pitch + at, half), :] = part
             return 0
 
+        def spread_rows(b):
+            here = pl.ds(b * 8 * half, 4 * half)
+            for side, source in enumerate((near, cross)):
+                value = jnp.dot(source[here, :], places[side, :, pl.ds(512, 128)], preferred_element_type=jnp.float32)
+                for k in range(4):
+                    rows[b * 8 + k, pl.ds(side * half, half), :] = value[k * half : (k + 1) * half]
+
         lax.fori_loop(0, 4, split, 0)
-        lax.fori_loop(0, 32 // n, spread_out, 0)
+        lax.fori_loop(0, 32 // n, spread_cols, 0)
+        for b in range(4):
+            spread_rows(b)
 
     def turn_field(j, target, r, f):
         row = spread(rows[r, pl.ds(f, 1), :])
@@ -191,6 +203,7 @@
         follow = first_block(tile_at(lax.rem(i + 1, TILES), last)[1])
         partner = [lax.rem(r + offset + s, 32) for s in range(4)]
         total = [acc[tile, a // 16, a % 16] for a in range(32)]
+        done = 0
         for f in range(FIELDS[j]):
             turned = [now[f, q] for q in range(2)]
             for s in range(4):
@@ -199,7 +212,9 @@
                     for q in range(2):
                         a = (g % 2) * 16 + (g // 2) * 8 + s * 2 + q
                         total[a] = total[a] + jnp.minimum(turned[q], other)
-            turn_field(j, later, follow, f)
+            while done < FIELDS[j] and done * (FIELDS[j] - 10) < (f + 1) * FIELDS[j]:
+                turn_field(j, later, follow, done)
+                done += 1
         for a in range(32):
             acc[tile, a // 16, a % 16] = total[a]
 
@@ -255,13 +270,13 @@
     with jax.named_scope("total"):
         lax.fori_loop(0, 4, total_one, 0)
         natural = turn[pl.ds(0, 32), :]
-        natural = jnp.concatenate([natural, jnp.concatenate([natural[4:], natural[:4]], axis=0)], axis=1)
-        top = natural.astype(jnp.bfloat16)
-        rest = (natural - top.astype(jnp.float32)).astype(jnp.bfloat16)
-        weight = places[:, pl.ds(0, 256)]
-        both = jnp.dot(top, weight, preferred_element_type=jnp.float32)
-        both = both + jnp.dot(rest, weight, preferred_element_type=jnp.float32)
-        turn[pl.ds(0, 32), :] = both[:, :128] + both[:, 128:]
+        shifted = jnp.concatenate([natural[4:], natural[:4]], axis=0)
+        both = jnp.zeros((32, 128), jnp.float32)
+        for side, value in enumerate(sides(natural, shifted)):
+            for part in parts(value):
+                weight = places[side, pl.ds(0, 128), pl.ds(512, 128)]
+                both = both + jnp.dot(part, weight, preferred_element_type=jnp.float32)
+        turn[pl.ds(0, 32), :] = both
 
     def pack_sums(tile, _):
         r = first_block(tile)
@@ -399,7 +414,7 @@
             pltpu.VMEM((64, 8192), f32),
             pltpu.VMEM((32, 128, 128), f32),
             pltpu.VMEM((32, 128, 128), f32),
-            pltpu.VMEM((256, 1280), jnp.bfloat16),
+            pltpu.VMEM((2, 256, 640), jnp.bfloat16),
             pltpu.VMEM((16 * MOST, 256), jnp.bfloat16),
             pltpu.VMEM((16 * MOST, 256), jnp.bfloat16),
             pltpu.VMEM((32, MOST, 128), f32),

time: 77.1 us -> 74.7 us (0.969)
  Pallas kernels: 74.8 us -> 72.4 us
    pallas_call x1, Pallas kernels: 74.8 us -> 72.4 us  [per_device(): pl.pallas_call(kernel, out_shape=jax.ShapeDtypeStruct((64, 128), f32), in...]
where the time goes in v3:
time: 74.7 us; the launch traced here: 74.5 us
  Pallas kernels  72.4 us (97%)
  local copies, waits for them, and re-layouts  1.38 us (2%)
    pallas_call x1, Pallas kernels, per_device(): pl.pallas_call(kernel, out_shape=jax.ShapeDtypeStruct((64, 128), f32), in...  72.4 us

profile of v3, /device:TPU:0, one launch (start us, length us, event | category | flops | bytes accessed | tf_op | source)
XLA Modules:
  0.0 74.5 jit_solution(2062922478685417607)
XLA Ops:
  0.7 72.4 %shard_map.28 = f32[64,128]{1,0:T(8,128)} custom-call(s32[1]{0:T(128)S(6)} %copy.4.section, f32[64,8192]{1,0:T(8,128)} %x_hbm.1), custom_call_target="tpu_custom_call" | custom-call | tf_op jit(solution)/shard_map/pallas_call | solution.py:408
  73.1 1.4 %copy.5 = f32[64,4,16]{0,2,1:T(8,128)} copy(f32[64,4,16]{0,2,1:T(8,128)} %bitcast.4) | data formatting | bytes 32768

commit v4 on v3

--- a/solution.py
+++ b/solution.py
@@ -46,14 +46,14 @@
     column = yh * 2 + yl
 
     def blk_peer(e):
-        return (lax.rem(z + e // 8, 4), lax.rem(yh + (e // 4) % 2, 2), lax.rem(x + e % 4, 4), yl, core)
+        return (lax.rem(z + lax.div(e, 8), 4), lax.rem(yh + lax.div(e, 4), 2), lax.rem(x + e, 4), yl, core)
 
     def plane_peer(e):
-        return (lax.rem(z + e // 4, 4), yh, lax.rem(x + e % 4, 4), yl, core)
+        return (lax.rem(z + lax.div(e, 4), 4), yh, lax.rem(x + e, 4), yl, core)
 
     def column_peer(d):
         y = lax.rem(column + d, 4)
-        return (z, y // 2, x, lax.rem(y, 2), core)
+        return (z, lax.div(y, 2), x, lax.rem(y, 2), core)
 
     other_core = (z, yh, x, yl, 1 - core)
 
@@ -123,12 +123,12 @@
         for j in range(1, ROUNDS):
             over_peers(lambda e: a_copy(j, e).start())
 
-    def tile_at(i, last=True):
-        e = sum(jnp.where(i == k, ORDER[k], 0) for k in range(TILES)) if last else i
-        return e, lax.rem(z + e // 4, 4) * 4 + lax.rem(x + e % 4, 4)
+    def tile_at(i):
+        e = sum(jnp.where(i == k, ORDER[k], 0) for k in range(TILES))
+        return e, lax.rem(z + lax.div(e, 4), 4) * 4 + lax.rem(x + e, 4)
 
     def first_block(tile):
-        return (tile // 4) * 8 + lax.rem(tile, 4)
+        return 2 * tile - lax.rem(tile, 4)
 
     def place():
         here = lax.broadcasted_iota(jnp.int32, (256, 128), 0) % 128
@@ -197,10 +197,12 @@
             target[f, q] = pltpu.roll(row, 64 * q, 1, stride=8, stride_axis=0)
 
     def work(j, i, now, later):
-        last = j == ROUNDS - 1
-        _, tile = tile_at(i, last)
-        r = first_block(tile)
-        follow = first_block(tile_at(lax.rem(i + 1, TILES), last)[1])
+        after = lax.rem(i + 1, TILES)
+        if j == ROUNDS - 1:
+            tile, after = tile_at(i)[1], tile_at(after)[1]
+        else:
+            tile = i
+        r, follow = first_block(tile), first_block(after)
         partner = [lax.rem(r + offset + s, 32) for s in range(4)]
         total = [acc[tile, a // 16, a % 16] for a in range(32)]
         done = 0
@@ -219,7 +221,7 @@
             acc[tile, a // 16, a % 16] = total[a]
 
     def first_turn(j):
-        r0 = first_block(tile_at(0, j == ROUNDS - 1)[1])
+        r0 = first_block(tile_at(0)[1] if j == ROUNDS - 1 else 0)
 
         def some(b, _):
             for f in range(32):

time: 74.7 us -> 74.2 us (level)
  no operation moved by 1% of the time
where the time goes in v4:
time: 74.2 us; the launch traced here: 74 us
  Pallas kernels  71.9 us (97%)
  local copies, waits for them, and re-layouts  1.38 us (2%)
    pallas_call x1, Pallas kernels, per_device(): pl.pallas_call(kernel, out_shape=jax.ShapeDtypeStruct((64, 128), f32), in...  71.9 us

profile of v4, /device:TPU:0, one launch (start us, length us, event | category | flops | bytes accessed | tf_op | source)
XLA Modules:
  0.0 74.0 jit_solution(4237528608147117400)
XLA Ops:
  0.7 71.9 %shard_map.28 = f32[64,128]{1,0:T(8,128)} custom-call(s32[1]{0:T(128)S(6)} %copy.4.section, f32[64,8192]{1,0:T(8,128)} %x_hbm.1), custom_call_target="tpu_custom_call" | custom-call | tf_op jit(solution)/shard_map/pallas_call | solution.py:410
  72.6 1.4 %copy.5 = f32[64,4,16]{0,2,1:T(8,128)} copy(f32[64,4,16]{0,2,1:T(8,128)} %bitcast.4) | data formatting | bytes 32768

commit v5 on v4

--- a/solution.py
+++ b/solution.py
@@ -15,7 +15,7 @@
 
 FAR_FIRST = sorted(range(1, 32), key=lambda e: (-hops(e), (e * 13) % 32))
 AXES = ("z", "yh", "x", "yl", "core")
-FIELDS = (32, 64, 32, 128)
+FIELDS = (32, 32, 64, 128)
 ROUNDS = len(FIELDS)
 START = [sum(FIELDS[:j]) // 2 for j in range(ROUNDS)]
 MOST = max(FIELDS)
@@ -151,10 +151,11 @@
         half = FIELDS[j] // 2
         pitch = FIELDS[j] + 8
         n = min(32, 1024 // half)
+        some = 4 if half > 32 else 8
 
         def split(b, _):
-            for k in range(8):
-                t = b * 8 + k
+            for k in range(some):
+                t = b * some + k
                 here = pl.ds(pl.multiple_of(t * half, 16), half)
                 this = got[t, pl.ds(START[j], half), :]
                 for target, value in zip((near, cross), sides(this, got[lax.rem(t + 4, 32), pl.ds(START[j], half), :])):
@@ -186,7 +187,7 @@
                 for k in range(4):
                     rows[b * 8 + k, pl.ds(side * half, half), :] = value[k * half : (k + 1) * half]
 
-        lax.fori_loop(0, 4, split, 0)
+        lax.fori_loop(0, 32 // some, split, 0)
         lax.fori_loop(0, 32 // n, spread_cols, 0)
         for b in range(4):
             spread_rows(b)
@@ -224,12 +225,12 @@
         r0 = first_block(tile_at(0)[1] if j == ROUNDS - 1 else 0)
 
         def some(b, _):
-            for f in range(32):
-                turn_field(j, roll_a, r0, b * 32 + f)
+            for f in range(min(FIELDS[j], 64)):
+                turn_field(j, roll_a, r0, b * 64 + f)
             return 0
 
         with jax.named_scope("first"):
-            lax.fori_loop(0, FIELDS[j] // 32, some, 0)
+            lax.fori_loop(0, max(FIELDS[j] // 64, 1), some, 0)
 
     def arrived(j):
         with jax.named_scope("got_wait"):

time: 74.2 us -> 74.4 us (level)
  no operation moved by 1% of the time
where the time goes in v5:
time: 74.4 us; the launch traced here: 74.2 us
  Pallas kernels  72.2 us (97%)
  local copies, waits for them, and re-layouts  1.38 us (2%)
    pallas_call x1, Pallas kernels, per_device(): pl.pallas_call(kernel, out_shape=jax.ShapeDtypeStruct((64, 128), f32), in...  72.2 us

profile of v5, /device:TPU:0, one launch (start us, length us, event | category | flops | bytes accessed | tf_op | source)
XLA Modules:
  0.0 74.2 jit_solution(9202385976658508067)
XLA Ops:
  0.7 72.2 %shard_map.28 = f32[64,128]{1,0:T(8,128)} custom-call(s32[1]{0:T(128)S(6)} %copy.4.section, f32[64,8192]{1,0:T(8,128)} %x_hbm.1), custom_call_target="tpu_custom_call" | custom-call | tf_op jit(solution)/shard_map/pallas_call | solution.py:411
  72.8 1.4 %copy.5 = f32[64,4,16]{0,2,1:T(8,128)} copy(f32[64,4,16]{0,2,1:T(8,128)} %bitcast.4) | data formatting | bytes 32768
